TPU v7x, 32 devices: a whole 2x2x4 slice. The times are simulated.
32 devices in a mesh: scen: 4 (over x, core), var: 8 (over z, y).
Axes of the slice: x: 2, y: 2, z: 4, core: 2. Of those that a mesh axis runs over, the one named last changes fastest.
Arguments:
- start_point: float32 [512, 65536], P('scen', 'var'), may hold values from -1 to 1
- multipliers: float32 [512, 65536], P('scen', 'var'), may hold values from -3 to 3
- cost: bfloat16 [512, 65536], P('scen', 'var'), may hold values from -6 to 6
- curvature: bfloat16 [512, 65536], P('scen', 'var'), may hold values from 0.5 to 2
- recourse_rhs: float32 [512, 512], P('scen'), may hold values from -12 to 12
- technology: bfloat16 [512, 65536], P(None, 'var'), may hold values from -0.0234375 to 0.0234375
- scenario_weight: float32 [512], P('scen'), may hold values from 1 to 30
- previous_mean: float32 [4, 65536], P(None, 'var'), may hold values from -1 to 1
- active: int32 [512, 512], P('scen', 'var'), may hold values 0 or 1
Outputs:
- iterate: float32 [512, 65536], P('scen', 'var')
- new_multipliers: float32 [512, 65536], P('scen', 'var')
- bundle_mean: float32 [4, 65536], P(None, 'var')
- primal_norm: float32 [], replicated
- dual_norm: float32 [], replicated
All inputs are finite; a program needn't handle non-finite values. No bound on the sum of `active` on one device may be relied on, other than what follows from the above.
Results may differ from a plain program's by a relative error of at most 0.0007.
Values sent between devices are 32-bit elements; how exact they have to be, the bound alone decides.
A program may use at most 64 MiB of HBM per device.

v0:
```python
import jax
import jax.numpy as jnp
from jax import lax
from jax.sharding import PartitionSpec as P

V = 65536
BLK = 128
STEPS = 8
highest = lax.Precision.HIGHEST
penalty = 1.0
recourse_scale = 4.0
stride = 0.2
epsilon = 1e-06


def from_partner(block, axis, bit):
    count = lax.axis_size(axis)
    route = []
    for low in range(count):
        high = low | 1 << bit
        if high != low and high < count:
            route += [(low, high), (high, low)]
    return lax.ppermute(block, axis, route)


def shards(
    start_point,
    multipliers,
    cost,
    curvature,
    recourse_rhs,
    technology,
    scenario_weight,
    previous_mean,
    active,
):
    scen_rows, var_cols = start_point.shape
    groups = previous_mean.shape[0]
    group_size = lax.axis_size("scen") // groups
    position = lax.axis_index("scen")
    my_node = position // group_size
    node_of = jnp.full((scen_rows,), my_node, jnp.int32)
    member = (node_of[:, None] == jnp.arange(groups, dtype=jnp.int32)[None, :]).astype(jnp.float32)
    bundle_mass = lax.psum(jnp.sum(member * scenario_weight[:, None], axis=0), "scen")
    anchor = jnp.dot(member, previous_mean, precision=highest, preferred_element_type=jnp.float32)
    linear = cost.astype(jnp.float32) + multipliers - penalty * anchor
    diagonal = curvature.astype(jnp.float32) + penalty
    active_mask = (active > 0)[:, :, None]
    iterate = start_point
    for sweep in range(STEPS):
        rounded = iterate.astype(jnp.bfloat16)
        partial_image = lax.dot_general(
            rounded, technology, (((1,), (1,)), ((), ())), preferred_element_type=jnp.float32
        )
        image = lax.psum(partial_image, "var")
        shortfall = (image - recourse_rhs).astype(jnp.bfloat16)
        pullback = jnp.dot(shortfall, technology, preferred_element_type=jnp.float32)
        stepped = jnp.clip(
            iterate - stride * (diagonal * iterate + linear + recourse_scale * pullback), -1.0, 1.0
        )
        blocked = jnp.where(
            active_mask, stepped.reshape(scen_rows, -1, BLK), iterate.reshape(scen_rows, -1, BLK)
        )
        iterate = blocked.reshape(scen_rows, var_cols)
    weighted = scenario_weight[:, None] * iterate
    normaliser = jnp.sum(bundle_mass) * V
    own_total = jnp.sum(weighted, axis=0, keepdims=True)
    for bit in range(group_size.bit_length() - 1):
        own_total = own_total + from_partner(own_total, "scen", bit)
    own_mass = jnp.sum(
        bundle_mass * (jnp.arange(groups, dtype=jnp.int32) == my_node).astype(jnp.float32)
    )
    mean_row = own_total / own_mass
    old_row = lax.dynamic_slice_in_dim(previous_mean, my_node, 1, 0)
    leader = (position % group_size == 0).astype(jnp.float32)
    centred = iterate - mean_row
    drift_part = leader * own_mass * jnp.sum((mean_row - old_row) ** 2)
    spread_part = jnp.sum(scenario_weight[:, None] * centred * centred)
    drift_sum, spread = lax.psum((drift_part, spread_part), ("scen", "var"))
    collected = lax.all_gather(mean_row, "scen", axis=0, tiled=True)
    bundle_mean = collected.reshape(groups, group_size, var_cols)[:, 0, :]
    primal_norm = jnp.sqrt(spread / normaliser + epsilon)
    dual_norm = penalty * jnp.sqrt(drift_sum / normaliser + epsilon)
    factor = penalty * jnp.sqrt(primal_norm / dual_norm)
    new_multipliers = multipliers + factor * centred
    return (iterate, new_multipliers, bundle_mean, primal_norm, dual_norm)


def solution(mesh):
    placed = (
        P("scen", "var"),
        P("scen", "var"),
        P("scen", "var"),
        P("scen", "var"),
        P("scen", None),
        P(None, "var"),
        P("scen"),
        P(None, "var"),
        P("scen", "var"),
    )
    return jax.shard_map(
        shards,
        mesh=mesh,
        in_specs=placed,
        out_specs=(P("scen", "var"), P("scen", "var"), P(None, "var"), P(), P()),
        check_vma=False,
    )
```

profile of v0, /device:TPU:0, one launch (start us, length us, event | category | flops | bytes accessed | tf_op | source)
XLA Modules:
  0.0 788.8 jit_solution(14389353718733308539)
XLA Ops:
  7.2 0.0 all-reduce.10.cloned.1.call-start
  7.2 8.3 %fusion.55 = f32[128,512]{1,0:T(8,128)} fusion(bf16[512,8192]{1,0:T(8,128)(2,1)} %param.14, f32[128,8192]{1,0:T(8,128)} %param.9), kind=kOutput, calls=%fused_computation.68 | convolution fusion | flops 1074790400 | bytes 12845056 | tf_op jit(solution)/shard_map/dot_general | solution.py:52
  15.5 0.0 all-reduce.10.cloned.1.call-update
  15.6 0.0 all-reduce.12.cloned.1.call-start
  15.7 0.1 copy.16
  15.8 0.0 copy-start.8
  15.8 6.9 convolution_subtract_fusion
  22.8 66.7 %all-reduce.10.cloned.1.call-done = f32[128,512]{1,0:T(8,128)} async-done(((f32[128,512]{1,0:T(8,128)}), f32[128,512]{1,0:T(8,128)}) %all-reduce.10.cloned.1.call-update) | async-done | bytes 262160 | tf_op jit(solution)/shard_map/psum | solution.py:55
  89.4 2.7 broadcast_in_dim.37
  92.2 0.0 slice-start.1
  92.2 9.2 %fusion.39 = f32[128,8192]{1,0:T(8,128)S(1)} fusion(f32[128,8192]{1,0:T(8,128)} %param.9, bf16[512,8192]{1,0:T(8,128)(2,1)} %param.14, f32[128,8192]{1,0:T(8,128)} %convolution_subtract_fusion, bf16[128,8192]{1,0:T(8,128)(2,1)S(1)} %copy-done, f32[128,512]{1,0:T(8,128)} %all-reduce.10.cloned.1.call-done, f32[128,512]{1,0:T(8,128)S(1)} %copy-done.8, ...), kind=kOutput, calls=%fused_computation.48 | convolution fusion | flops 1084358656 | bytes 24641536 | tf_op jit(solution)/shard_map/dot_general | solution.py:57
  101.4 0.0 copy-start.7
  101.4 2.0 copy-done.7
  103.4 3.6 fusion.53
  107.0 0.0 all-reduce.12.cloned.1.call-update
  107.1 0.2 all-reduce.14.cloned.1.call-start
  107.3 70.2 %all-reduce.12.cloned.1.call-done = f32[128,512]{1,0:T(8,128)} async-done(((f32[128,512]{1,0:T(8,128)}), f32[128,512]{1,0:T(8,128)}) %all-reduce.12.cloned.1.call-update) | async-done | bytes 262160 | tf_op jit(solution)/shard_map/psum | solution.py:55
  177.5 9.0 %fusion.37 = f32[128,8192]{1,0:T(8,128)S(1)} fusion(f32[128,8192]{1,0:T(8,128)} %copy-done.7, bf16[512,8192]{1,0:T(8,128)(2,1)} %param.14, f32[128,8192]{1,0:T(8,128)} %convolution_subtract_fusion, bf16[128,8192]{1,0:T(8,128)(2,1)S(1)} %copy-done, f32[128,512]{1,0:T(8,128)} %all-reduce.12.cloned.1.call-done, f32[128,512]{1,0:T(8,128)S(1)} %copy-done.8, ...), kind=kOutput, calls=%fused_computation.46 | convolution fusion | flops 1084358656 | bytes 24641536 | tf_op jit(solution)/shard_map/dot_general | solution.py:57
  186.5 0.0 copy-start.2
  186.5 2.0 copy-done.2
  188.5 7.0 fusion.51
  195.5 0.0 all-reduce.14.cloned.1.call-update
  195.6 0.0 all-reduce.16.cloned.1.call-start
  195.6 70.3 %all-reduce.14.cloned.1.call-done = f32[128,512]{1,0:T(8,128)} async-done(((f32[128,512]{1,0:T(8,128)}), f32[128,512]{1,0:T(8,128)}) %all-reduce.14.cloned.1.call-update) | async-done | bytes 262160 | tf_op jit(solution)/shard_map/psum | solution.py:55
  265.9 9.0 %fusion.35 = f32[128,8192]{1,0:T(8,128)S(1)} fusion(f32[128,8192]{1,0:T(8,128)} %copy-done.2, bf16[512,8192]{1,0:T(8,128)(2,1)} %param.14, f32[128,8192]{1,0:T(8,128)} %convolution_subtract_fusion, bf16[128,8192]{1,0:T(8,128)(2,1)S(1)} %copy-done, f32[128,512]{1,0:T(8,128)} %all-reduce.14.cloned.1.call-done, f32[128,512]{1,0:T(8,128)S(1)} %copy-done.8, ...), kind=kOutput, calls=%fused_computation.44 | convolution fusion | flops 1084358656 | bytes 24641536 | tf_op jit(solution)/shard_map/dot_general | solution.py:57
  275.0 2.0 copy-done.3
  277.0 7.0 fusion.49
  284.0 0.0 all-reduce.16.cloned.1.call-update
  284.0 0.3 all-reduce.18.cloned.1.call-start
  284.3 70.1 %all-reduce.16.cloned.1.call-done = f32[128,512]{1,0:T(8,128)} async-done(((f32[128,512]{1,0:T(8,128)}), f32[128,512]{1,0:T(8,128)}) %all-reduce.16.cloned.1.call-update) | async-done | bytes 262160 | tf_op jit(solution)/shard_map/psum | solution.py:55
  354.4 9.0 %fusion.33 = f32[128,8192]{1,0:T(8,128)S(1)} fusion(f32[128,8192]{1,0:T(8,128)} %copy-done.3, bf16[512,8192]{1,0:T(8,128)(2,1)} %param.14, f32[128,8192]{1,0:T(8,128)} %convolution_subtract_fusion, bf16[128,8192]{1,0:T(8,128)(2,1)S(1)} %copy-done, f32[128,512]{1,0:T(8,128)} %all-reduce.16.cloned.1.call-done, f32[128,512]{1,0:T(8,128)S(1)} %copy-done.8, ...), kind=kOutput, calls=%fused_computation.42 | convolution fusion | flops 1084358656 | bytes 24641536 | tf_op jit(solution)/shard_map/dot_general | solution.py:57
  363.4 2.0 copy-done.4
  365.4 7.0 fusion.47
  372.4 0.0 all-reduce.18.cloned.1.call-update
  372.5 0.0 all-reduce.20.cloned.1.call-start
  372.5 70.4 %all-reduce.18.cloned.1.call-done = f32[128,512]{1,0:T(8,128)} async-done(((f32[128,512]{1,0:T(8,128)}), f32[128,512]{1,0:T(8,128)}) %all-reduce.18.cloned.1.call-update) | async-done | bytes 262160 | tf_op jit(solution)/shard_map/psum | solution.py:55
  442.9 9.0 %fusion.31 = f32[128,8192]{1,0:T(8,128)S(1)} fusion(f32[128,8192]{1,0:T(8,128)} %copy-done.4, bf16[512,8192]{1,0:T(8,128)(2,1)} %param.14, f32[128,8192]{1,0:T(8,128)} %convolution_subtract_fusion, bf16[128,8192]{1,0:T(8,128)(2,1)S(1)} %copy-done, f32[128,512]{1,0:T(8,128)} %all-reduce.18.cloned.1.call-done, f32[128,512]{1,0:T(8,128)S(1)} %copy-done.8, ...), kind=kOutput, calls=%fused_computation.40 | convolution fusion | flops 1084358656 | bytes 24641536 | tf_op jit(solution)/shard_map/dot_general | solution.py:57
  451.9 2.0 copy-done.5
  453.9 7.0 fusion.45
  460.9 0.0 all-reduce.20.cloned.1.call-update
  461.0 0.4 all-reduce.22.cloned.1.call-start
  461.4 69.9 %all-reduce.20.cloned.1.call-done = f32[128,512]{1,0:T(8,128)} async-done(((f32[128,512]{1,0:T(8,128)}), f32[128,512]{1,0:T(8,128)}) %all-reduce.20.cloned.1.call-update) | async-done | bytes 262160 | tf_op jit(solution)/shard_map/psum | solution.py:55
  531.4 9.0 %fusion.29 = f32[128,8192]{1,0:T(8,128)S(1)} fusion(f32[128,8192]{1,0:T(8,128)} %copy-done.5, bf16[512,8192]{1,0:T(8,128)(2,1)} %param.14, f32[128,8192]{1,0:T(8,128)} %convolution_subtract_fusion, bf16[128,8192]{1,0:T(8,128)(2,1)S(1)} %copy-done, f32[128,512]{1,0:T(8,128)} %all-reduce.20.cloned.1.call-done, f32[128,512]{1,0:T(8,128)S(1)} %copy-done.8, ...), kind=kOutput, calls=%fused_computation.38 | convolution fusion | flops 1084358656 | bytes 24641536 | tf_op jit(solution)/shard_map/dot_general | solution.py:57
  540.4 2.0 copy-done.6
  542.4 7.0 fusion.43
  549.4 0.0 all-reduce.22.cloned.1.call-update
  549.4 0.0 all-reduce.24.cloned.1.call-start
  549.5 70.3 %all-reduce.22.cloned.1.call-done = f32[128,512]{1,0:T(8,128)} async-done(((f32[128,512]{1,0:T(8,128)}), f32[128,512]{1,0:T(8,128)}) %all-reduce.22.cloned.1.call-update) | async-done | bytes 262160 | tf_op jit(solution)/shard_map/psum | solution.py:55
  619.8 9.0 %fusion.27 = f32[128,8192]{1,0:T(8,128)S(1)} fusion(f32[128,8192]{1,0:T(8,128)} %copy-done.6, bf16[512,8192]{1,0:T(8,128)(2,1)} %param.14, f32[128,8192]{1,0:T(8,128)} %convolution_subtract_fusion, bf16[128,8192]{1,0:T(8,128)(2,1)S(1)} %copy-done, f32[128,512]{1,0:T(8,128)} %all-reduce.22.cloned.1.call-done, f32[128,512]{1,0:T(8,128)S(1)} %copy-done.8, ...), kind=kOutput, calls=%fused_computation.36 | convolution fusion | flops 1084358656 | bytes 24641536 | tf_op jit(solution)/shard_map/dot_general | solution.py:57
  628.8 2.0 copy-done.1
  630.8 7.0 fusion.41
  637.9 0.0 all-reduce.24.cloned.1.call-update
  637.9 0.2 multiply_reduce_fusion.2
  638.1 5.8 psum.85
  643.9 0.6 fusion.60
  645.2 63.1 %all-reduce.24.cloned.1.call-done = f32[128,512]{1,0:T(8,128)} async-done(((f32[128,512]{1,0:T(8,128)}), f32[128,512]{1,0:T(8,128)}) %all-reduce.24.cloned.1.call-update) | async-done | bytes 262160 | tf_op jit(solution)/shard_map/psum | solution.py:55
  708.3 11.2 %multiply_reduce_fusion = (f32[8192]{0:T(1024)S(1)}, f32[128,8192]{1,0:T(8,128)}) fusion(f32[128]{0:T(128)S(1)} %copy-done.11, f32[128,8192]{1,0:T(8,128)} %copy-done.1, bf16[512,8192]{1,0:T(8,128)(2,1)} %param.14, f32[128,512]{1,0:T(8,128)} %all-reduce.24.cloned.1.call-done, f32[128,512]{1,0:T(8,128)S(1)} %copy-done.8, ...), kind=kOutput, calls=%fused_computation.52 | convolution fusion | flops 1086447616 | bytes 24674816 | tf_op jit(solution)/shard_map/dot_general | solution.py:57
  719.5 0.7 broadcast_divide_fusion
  720.2 0.7 multiply_reduce_fusion.1
  722.1 3.9 fusion.40
  726.1 5.4 all-gather
  731.5 39.7 %all-reduce = (f32[]{:T(128)}, f32[]{:T(128)}) all-reduce(f32[]{:T(128)} %fusion.40, f32[]{:T(128)S(6)} %mul.145), channel_id=1, replica_groups=mesh['scen'=4,'var'=8] {'scen','var'}, use_global_device_ids=true, to_apply=%region_13.14 | all-reduce | flops 2 | bytes 16 | tf_op jit(solution)/shard_map/psum | solution.py:79
  772.7 6.1 multiply_add_fusion
  778.8 0.7 reshape.75
  (21 shorter events, 0.1 us)
Async XLA Ops:
  7.2 8.5 %copy-start.10 = (s32[128,64]{0,1:T(8,128)S(1)}, s32[128,64]{0,1:T(8,128)}, u32[]{:S(2)}) copy-start(s32[128,64]{0,1:T(8,128)} %param.17) | copy-start | bytes 98308
  7.2 8.6 %copy-start.9 = (f32[4,8192]{1,0:T(4,128)S(1)}, f32[4,8192]{1,0:T(4,128)}, u32[]{:S(2)}) copy-start(f32[4,8192]{1,0:T(4,128)} %param.16) | copy-start | bytes 393220
  7.2 82.3 %all-reduce.10.cloned.1.call-start = ((), (), s32[]{:S(2)}) async-start(), calls=%async_computation | async-start | bytes 524288 | tf_op jit(solution)/shard_map/psum | solution.py:55
  15.6 161.9 %all-reduce.12.cloned.1.call-start = ((), (), s32[]{:S(2)}) async-start(), calls=%async_computation.1 | async-start | bytes 524288 | tf_op jit(solution)/shard_map/psum | solution.py:55
  15.8 76.4 %copy-start = (bf16[128,8192]{1,0:T(8,128)(2,1)S(1)}, bf16[128,8192]{1,0:T(8,128)(2,1)}, u32[]{:S(2)}) copy-start(bf16[128,8192]{1,0:T(8,128)(2,1)} %param.12) | copy-start | bytes 6291460
  15.8 76.4 %copy-start.8 = (f32[128,512]{1,0:T(8,128)S(1)}, f32[128,512]{1,0:T(8,128)}, u32[]{:S(2)}) copy-start(f32[128,512]{1,0:T(8,128)} %param.13) | copy-start | bytes 786436
  89.4 14.0 %slice-start = ((s8[8388608]{0:T(1024)(128)(4,1)}), s8[4194304]{0:T(1024)(128)(4,1)S(1)}, s32[]{:S(2)}) async-start(s8[8388608]{0:T(1024)(128)(4,1)} %bitcast.28), calls=%async_computation.8 | async-start | bytes 8388608
  92.2 11.2 %slice-start.1 = ((s8[8388608]{0:T(1024)(128)(4,1)}), s8[4194304]{0:T(1024)(128)(4,1)S(1)}, s32[]{:S(2)}) async-start(s8[8388608]{0:T(1024)(128)(4,1)} %bitcast.28), calls=%async_computation.9 | async-start | bytes 8388608
  101.4 2.0 copy-start.7
  107.1 158.9 %all-reduce.14.cloned.1.call-start = ((), (), s32[]{:S(2)}) async-start(), calls=%async_computation.2 | async-start | bytes 524288 | tf_op jit(solution)/shard_map/psum | solution.py:55
  186.5 2.0 copy-start.2
  195.6 158.8 %all-reduce.16.cloned.1.call-start = ((), (), s32[]{:S(2)}) async-start(), calls=%async_computation.3 | async-start | bytes 524288 | tf_op jit(solution)/shard_map/psum | solution.py:55
  274.9 2.0 copy-start.3
  284.0 158.9 %all-reduce.18.cloned.1.call-start = ((), (), s32[]{:S(2)}) async-start(), calls=%async_computation.4 | async-start | bytes 524288 | tf_op jit(solution)/shard_map/psum | solution.py:55
  363.4 2.0 copy-start.4
  372.5 158.9 %all-reduce.20.cloned.1.call-start = ((), (), s32[]{:S(2)}) async-start(), calls=%async_computation.5 | async-start | bytes 524288 | tf_op jit(solution)/shard_map/psum | solution.py:55
  451.9 2.0 copy-start.5
  461.0 158.8 %all-reduce.22.cloned.1.call-start = ((), (), s32[]{:S(2)}) async-start(), calls=%async_computation.6 | async-start | bytes 524288 | tf_op jit(solution)/shard_map/psum | solution.py:55
  540.4 2.0 copy-start.6
  549.4 158.8 %all-reduce.24.cloned.1.call-start = ((), (), s32[]{:S(2)}) async-start(), calls=%async_computation.7 | async-start | bytes 524288 | tf_op jit(solution)/shard_map/psum | solution.py:55
  628.8 2.0 copy-start.1
  630.8 7.1 copy-start.11
Sparse Core Ops, SparseCore 0:
  15.7 73.7 all-reduce.9
  107.2 70.2 all-reduce.11
  195.7 70.1 all-reduce.13
  284.1 70.2 all-reduce.15
  372.6 70.2 all-reduce.17
  461.1 70.2 all-reduce.19
  549.6 70.1 all-reduce.21
  638.0 70.2 all-reduce.23
where the time goes:
time: 796 us; the launch traced here: 789 us
  waiting for transfers between devices  551 us (69%)
  matrix products  135 us (17%)
  blocking collectives  50.9 us (6%)
  between operations  20.3 us (3%)
  local copies, waits for them, and re-layouts  17.6 us (2%)
  other arithmetic  12.2 us (2%)
    psum x8, waiting for transfers between devices, shards(): image = lax.psum(partial_image, 'var')  551 us
    dot_general x8, matrix products, shards(): jnp.dot(shortfall, technology, preferred_element_type=jnp.float32)  74.5 us
    dot_general x8, matrix products, shards(): lax.dot_general(rounded, technology, (((1,), (1,)), ((), ())), preferred_...  54 us
    psum x1, blocking collectives, shards(): drift_sum, spread = lax.psum((drift_part, spread_part), ('scen', 'var'))  39.7 us
  transfers between devices with their start and end apart: 8, of which 8 were waited for; matrix products, arithmetic and copies ran while one was open for 1% of the time, Pallas kernels for 0%

commit v1 on v0

--- a/solution.py
+++ b/solution.py
@@ -52,7 +52,9 @@
         partial_image = lax.dot_general(
             rounded, technology, (((1,), (1,)), ((), ())), preferred_element_type=jnp.float32
         )
-        image = lax.psum(partial_image, "var")
+        image = partial_image
+        for hop in (1, 2, 4):
+            image = image + lax.ppermute(image, "var", [(dev, dev ^ hop) for dev in range(8)])
         shortfall = (image - recourse_rhs).astype(jnp.bfloat16)
         pullback = jnp.dot(shortfall, technology, preferred_element_type=jnp.float32)
         stepped = jnp.clip(

time: 796 us -> 371 us (0.47)
  waiting for transfers between devices: 551 us -> 165 us
  matrix products: 135 us -> 71.5 us
  starting transfers between devices: 1.12 us -> 53.4 us
  local copies, waits for them, and re-layouts: 17.6 us -> 3.61 us
  between operations: 20.3 us -> 6.92 us
    psum x8 -> x0, waiting for transfers between devices: 551 us -> none  [shards(): image = lax.psum(partial_image, 'var')]
    ppermute x0 -> x24, waiting for transfers between devices: none -> 165 us  [shards(): lax.ppermute(image, 'var', [(dev, dev ^ hop) for dev in range(8)])]
    ppermute x0 -> x24, starting transfers between devices: none -> 53.4 us  [shards(): lax.ppermute(image, 'var', [(dev, dev ^ hop) for dev in range(8)])]
    dot_general x8, matrix products: 74.5 us -> 38.1 us  [shards(): jnp.dot(shortfall, technology, preferred_element_type=jnp.float32)]
    dot_general x8, matrix products: 54 us -> 28.2 us  [shards(): lax.dot_general(rounded, technology, (((1,), (1,)), ((), ())), preferred_...]
    unnamed x28 -> x18, local copies, waits for them, and re-layouts: 14.1 us -> 0.05 us
  transfers between devices with their start and end apart: 8 -> 24, of which waited for: 8 -> 24; matrix products, arithmetic and copies ran while one was open for 1% -> 2% of each run, Pallas kernels for 0% -> 0%
where the time goes in v1:
time: 371 us; the launch traced here: 366 us
  waiting for transfers between devices  165 us (44%)
  matrix products  71.5 us (19%)
  starting transfers between devices  53.4 us (14%)
  blocking collectives  51.4 us (14%)
  other arithmetic  13.4 us (4%)
  between operations  6.92 us (2%)
    ppermute x24, waiting for transfers between devices, shards(): lax.ppermute(image, 'var', [(dev, dev ^ hop) for dev in range(8)])  165 us
    ppermute x24, starting transfers between devices, shards(): lax.ppermute(image, 'var', [(dev, dev ^ hop) for dev in range(8)])  53.4 us
    psum x1, blocking collectives, shards(): drift_sum, spread = lax.psum((drift_part, spread_part), ('scen', 'var'))  40 us
    dot_general x8, matrix products, shards(): jnp.dot(shortfall, technology, preferred_element_type=jnp.float32)  38.1 us
    dot_general x8, matrix products, shards(): lax.dot_general(rounded, technology, (((1,), (1,)), ((), ())), preferred_...  28.2 us
  transfers between devices with their start and end apart: 24, of which 24 were waited for; matrix products, arithmetic and copies ran while one was open for 2% of the time, Pallas kernels for 0%

profile of v1, /device:TPU:0, one launch (start us, length us, event | category | flops | bytes accessed | tf_op | source)
XLA Modules:
  0.0 365.6 jit_solution(14511669831723710123)
XLA Ops:
  0.7 7.6 %fusion.55 = f32[128,512]{1,0:T(8,128)S(1)} fusion(bf16[512,8192]{1,0:T(8,128)(2,1)} %param.14, f32[128,8192]{1,0:T(8,128)} %param.9), kind=kOutput, calls=%fused_computation.68 | convolution fusion | flops 1074790400 | bytes 12845056 | tf_op jit(solution)/shard_map/dot_general | solution.py:52
  8.3 3.1 collective-permute-start
  11.3 6.3 %collective-permute-done = f32[128,512]{1,0:T(8,128)S(1)} collective-permute-done((f32[128,512]{1,0:T(8,128)S(1)}, f32[128,512]{1,0:T(8,128)S(1)}, u32[]{:S(2)}, u32[]{:S(2)}) %collective-permute-start) | collective-permute-done | bytes 262176 | tf_op jit(solution)/shard_map/ppermute | solution.py:57
  17.7 1.9 collective-permute-start.1
  19.7 5.5 %collective-permute-done.1 = f32[128,512]{1,0:T(8,128)S(1)} collective-permute-done((f32[128,512]{1,0:T(8,128)S(1)}, f32[128,512]{1,0:T(8,128)S(1)}, u32[]{:S(2)}, u32[]{:S(2)}) %collective-permute-start.1) | collective-permute-done | bytes 262176 | tf_op jit(solution)/shard_map/ppermute | solution.py:57
  25.3 2.6 collective-permute-start.2
  27.9 5.2 %convolution_subtract_fusion = f32[128,8192]{1,0:T(8,128)S(1)} fusion(f32[4,8192]{1,0:T(4,128)S(1)} %copy-done.6, f32[128,8192]{1,0:T(8,128)} %param.10, bf16[128,8192]{1,0:T(8,128)(2,1)} %param.11, pred[4]{0:T(512)(128)(4,1)S(1)} %iota_compare_fusion), kind=kOutput, calls=%fused_computation.24 | convolution fusion | flops 53477376 | bytes 10616836 | tf_op jit(solution)/shard_map/dot_general | solution.py:45
  33.1 5.4 %collective-permute-done.2 = f32[128,512]{1,0:T(8,128)S(1)} collective-permute-done((f32[128,512]{1,0:T(8,128)S(1)}, f32[128,512]{1,0:T(8,128)S(1)}, u32[]{:S(2)}, u32[]{:S(2)}) %collective-permute-start.2) | collective-permute-done | bytes 262176 | tf_op jit(solution)/shard_map/ppermute | solution.py:57
  38.5 2.7 broadcast_in_dim.37
  41.2 5.2 %fusion.39 = f32[128,8192]{1,0:T(8,128)S(1)} fusion(f32[128,8192]{1,0:T(8,128)} %param.9, bf16[512,8192]{1,0:T(8,128)(2,1)S(1)} %copy-done, f32[128,8192]{1,0:T(8,128)S(1)} %convolution_subtract_fusion, bf16[128,8192]{1,0:T(8,128)(2,1)S(1)} %copy-done.2, f32[128,512]{1,0:T(8,128)S(1)} %copy-done.5, f32[128,512]{1,0:T(8,128)S(1)} %add.152, ...), kind=kOutput, calls=%fused_computation.48 | convolution fusion | flops 1084424192 | bytes 24903680 | tf_op jit(solution)/shard_map/dot_general | solution.py:59
  46.5 2.9 fusion.53
  50.6 6.4 %collective-permute-done.3 = f32[128,512]{1,0:T(8,128)S(1)} collective-permute-done((f32[128,512]{1,0:T(8,128)S(1)}, f32[128,512]{1,0:T(8,128)S(1)}, u32[]{:S(2)}, u32[]{:S(2)}) %collective-permute-start.3) | collective-permute-done | bytes 262176 | tf_op jit(solution)/shard_map/ppermute | solution.py:57
  58.1 5.7 %collective-permute-done.4 = f32[128,512]{1,0:T(8,128)S(1)} collective-permute-done((f32[128,512]{1,0:T(8,128)S(1)}, f32[128,512]{1,0:T(8,128)S(1)}, u32[]{:S(2)}, u32[]{:S(2)}) %collective-permute-start.4) | collective-permute-done | bytes 262176 | tf_op jit(solution)/shard_map/ppermute | solution.py:57
  63.8 3.4 collective-permute-start.5
  67.2 10.7 %collective-permute-done.5 = f32[128,512]{1,0:T(8,128)S(1)} collective-permute-done((f32[128,512]{1,0:T(8,128)S(1)}, f32[128,512]{1,0:T(8,128)S(1)}, u32[]{:S(2)}, u32[]{:S(2)}) %collective-permute-start.5) | collective-permute-done | bytes 262176 | tf_op jit(solution)/shard_map/ppermute | solution.py:57
  77.9 3.3 fusion.37
  81.2 2.9 fusion.51
  85.7 5.8 %collective-permute-done.6 = f32[128,512]{1,0:T(8,128)S(1)} collective-permute-done((f32[128,512]{1,0:T(8,128)S(1)}, f32[128,512]{1,0:T(8,128)S(1)}, u32[]{:S(2)}, u32[]{:S(2)}) %collective-permute-start.6) | collective-permute-done | bytes 262176 | tf_op jit(solution)/shard_map/ppermute | solution.py:57
  91.6 1.7 collective-permute-start.7
  93.2 5.6 %collective-permute-done.7 = f32[128,512]{1,0:T(8,128)S(1)} collective-permute-done((f32[128,512]{1,0:T(8,128)S(1)}, f32[128,512]{1,0:T(8,128)S(1)}, u32[]{:S(2)}, u32[]{:S(2)}) %collective-permute-start.7) | collective-permute-done | bytes 262176 | tf_op jit(solution)/shard_map/ppermute | solution.py:57
  98.9 3.5 collective-permute-start.8
  102.4 10.7 %collective-permute-done.8 = f32[128,512]{1,0:T(8,128)S(1)} collective-permute-done((f32[128,512]{1,0:T(8,128)S(1)}, f32[128,512]{1,0:T(8,128)S(1)}, u32[]{:S(2)}, u32[]{:S(2)}) %collective-permute-start.8) | collective-permute-done | bytes 262176 | tf_op jit(solution)/shard_map/ppermute | solution.py:57
  113.0 3.3 fusion.35
  116.3 3.1 fusion.49
  121.0 5.8 %collective-permute-done.9 = f32[128,512]{1,0:T(8,128)S(1)} collective-permute-done((f32[128,512]{1,0:T(8,128)S(1)}, f32[128,512]{1,0:T(8,128)S(1)}, u32[]{:S(2)}, u32[]{:S(2)}) %collective-permute-start.9) | collective-permute-done | bytes 262176 | tf_op jit(solution)/shard_map/ppermute | solution.py:57
  126.9 1.7 collective-permute-start.10
  128.6 5.6 %collective-permute-done.10 = f32[128,512]{1,0:T(8,128)S(1)} collective-permute-done((f32[128,512]{1,0:T(8,128)S(1)}, f32[128,512]{1,0:T(8,128)S(1)}, u32[]{:S(2)}, u32[]{:S(2)}) %collective-permute-start.10) | collective-permute-done | bytes 262176 | tf_op jit(solution)/shard_map/ppermute | solution.py:57
  134.2 3.4 collective-permute-start.11
  137.6 10.7 %collective-permute-done.11 = f32[128,512]{1,0:T(8,128)S(1)} collective-permute-done((f32[128,512]{1,0:T(8,128)S(1)}, f32[128,512]{1,0:T(8,128)S(1)}, u32[]{:S(2)}, u32[]{:S(2)}) %collective-permute-start.11) | collective-permute-done | bytes 262176 | tf_op jit(solution)/shard_map/ppermute | solution.py:57
  148.3 3.3 fusion.33
  151.6 2.9 fusion.47
  156.1 5.8 %collective-permute-done.12 = f32[128,512]{1,0:T(8,128)S(1)} collective-permute-done((f32[128,512]{1,0:T(8,128)S(1)}, f32[128,512]{1,0:T(8,128)S(1)}, u32[]{:S(2)}, u32[]{:S(2)}) %collective-permute-start.12) | collective-permute-done | bytes 262176 | tf_op jit(solution)/shard_map/ppermute | solution.py:57
  161.9 1.7 collective-permute-start.13
  163.6 5.6 %collective-permute-done.13 = f32[128,512]{1,0:T(8,128)S(1)} collective-permute-done((f32[128,512]{1,0:T(8,128)S(1)}, f32[128,512]{1,0:T(8,128)S(1)}, u32[]{:S(2)}, u32[]{:S(2)}) %collective-permute-start.13) | collective-permute-done | bytes 262176 | tf_op jit(solution)/shard_map/ppermute | solution.py:57
  169.3 3.4 collective-permute-start.14
  172.7 10.7 %collective-permute-done.14 = f32[128,512]{1,0:T(8,128)S(1)} collective-permute-done((f32[128,512]{1,0:T(8,128)S(1)}, f32[128,512]{1,0:T(8,128)S(1)}, u32[]{:S(2)}, u32[]{:S(2)}) %collective-permute-start.14) | collective-permute-done | bytes 262176 | tf_op jit(solution)/shard_map/ppermute | solution.py:57
  183.4 3.3 fusion.31
  186.7 2.9 fusion.45
  191.2 5.8 %collective-permute-done.15 = f32[128,512]{1,0:T(8,128)S(1)} collective-permute-done((f32[128,512]{1,0:T(8,128)S(1)}, f32[128,512]{1,0:T(8,128)S(1)}, u32[]{:S(2)}, u32[]{:S(2)}) %collective-permute-start.15) | collective-permute-done | bytes 262176 | tf_op jit(solution)/shard_map/ppermute | solution.py:57
  197.0 1.7 collective-permute-start.16
  198.7 5.6 %collective-permute-done.16 = f32[128,512]{1,0:T(8,128)S(1)} collective-permute-done((f32[128,512]{1,0:T(8,128)S(1)}, f32[128,512]{1,0:T(8,128)S(1)}, u32[]{:S(2)}, u32[]{:S(2)}) %collective-permute-start.16) | collective-permute-done | bytes 262176 | tf_op jit(solution)/shard_map/ppermute | solution.py:57
  204.4 3.4 collective-permute-start.17
  207.8 10.7 %collective-permute-done.17 = f32[128,512]{1,0:T(8,128)S(1)} collective-permute-done((f32[128,512]{1,0:T(8,128)S(1)}, f32[128,512]{1,0:T(8,128)S(1)}, u32[]{:S(2)}, u32[]{:S(2)}) %collective-permute-start.17) | collective-permute-done | bytes 262176 | tf_op jit(solution)/shard_map/ppermute | solution.py:57
  218.5 3.5 fusion.29
  222.0 2.9 fusion.43
  224.9 1.6 collective-permute-start.18
  226.5 5.8 %collective-permute-done.18 = f32[128,512]{1,0:T(8,128)S(1)} collective-permute-done((f32[128,512]{1,0:T(8,128)S(1)}, f32[128,512]{1,0:T(8,128)S(1)}, u32[]{:S(2)}, u32[]{:S(2)}) %collective-permute-start.18) | collective-permute-done | bytes 262176 | tf_op jit(solution)/shard_map/ppermute | solution.py:57
  232.4 1.7 collective-permute-start.19
  234.0 5.6 %collective-permute-done.19 = f32[128,512]{1,0:T(8,128)S(1)} collective-permute-done((f32[128,512]{1,0:T(8,128)S(1)}, f32[128,512]{1,0:T(8,128)S(1)}, u32[]{:S(2)}, u32[]{:S(2)}) %collective-permute-start.19) | collective-permute-done | bytes 262176 | tf_op jit(solution)/shard_map/ppermute | solution.py:57
  239.7 3.4 collective-permute-start.20
  243.2 10.7 %collective-permute-done.20 = f32[128,512]{1,0:T(8,128)S(1)} collective-permute-done((f32[128,512]{1,0:T(8,128)S(1)}, f32[128,512]{1,0:T(8,128)S(1)}, u32[]{:S(2)}, u32[]{:S(2)}) %collective-permute-start.20) | collective-permute-done | bytes 262176 | tf_op jit(solution)/shard_map/ppermute | solution.py:57
  253.8 4.7 %fusion.27 = f32[128,8192]{1,0:T(8,128)S(1)} fusion(f32[128,8192]{1,0:T(8,128)} %copy-done.4, bf16[512,8192]{1,0:T(8,128)(2,1)S(1)} %copy-done, f32[128,8192]{1,0:T(8,128)S(1)} %convolution_subtract_fusion, bf16[128,8192]{1,0:T(8,128)(2,1)S(1)} %copy-done.2, f32[128,512]{1,0:T(8,128)S(1)} %copy-done.5, f32[128,512]{1,0:T(8,128)S(1)} %add.182, ...), kind=kOutput, calls=%fused_computation.36 | convolution fusion | flops 1084424192 | bytes 24903680 | tf_op jit(solution)/shard_map/dot_general | solution.py:59
  258.6 2.9 fusion.41
  263.1 5.8 %collective-permute-done.21 = f32[128,512]{1,0:T(8,128)S(1)} collective-permute-done((f32[128,512]{1,0:T(8,128)S(1)}, f32[128,512]{1,0:T(8,128)S(1)}, u32[]{:S(2)}, u32[]{:S(2)}) %collective-permute-start.21) | collective-permute-done | bytes 262176 | tf_op jit(solution)/shard_map/ppermute | solution.py:57
  269.0 1.7 collective-permute-start.22
  270.6 5.6 %collective-permute-done.22 = f32[128,512]{1,0:T(8,128)S(1)} collective-permute-done((f32[128,512]{1,0:T(8,128)S(1)}, f32[128,512]{1,0:T(8,128)S(1)}, u32[]{:S(2)}, u32[]{:S(2)}) %collective-permute-start.22) | collective-permute-done | bytes 262176 | tf_op jit(solution)/shard_map/ppermute | solution.py:57
  277.0 3.4 collective-permute-start.23
  280.6 5.9 %psum.21 = f32[4]{0:T(128)S(1)} all-reduce(f32[4]{0:T(128)S(1)} %multiply_reduce_fusion.2), channel_id=1, replica_groups=mesh['scen'=4,'var'=8] {'scen'}, use_global_device_ids=true, to_apply=%region_2.3 | all-reduce | flops 4 | bytes 32 | tf_op jit(solution)/shard_map/psum | solution.py:44
  287.7 3.6 collective-permute-done.23
  291.4 11.4 %multiply_reduce_fusion = (f32[8192]{0:T(1024)S(1)}, f32[128,8192]{1,0:T(8,128)}) fusion(f32[128]{0:T(128)S(1)} %copy-done.8, f32[128,8192]{1,0:T(8,128)} %copy-done.3, bf16[512,8192]{1,0:T(8,128)(2,1)} %param.14, f32[128,512]{1,0:T(8,128)S(1)} %copy-done.5, f32[128,512]{1,0:T(8,128)} %add.187, f32[128,512]{1,0:T(8,128)} %collective-permute-done.23, ...), kind=kOutput, calls=%fused_computation.52 | convolution fusion | flops 1086513152 | bytes 24936960 | tf_op jit(solution)/shard_map/dot_general | solution.py:59
  305.4 3.9 %fusion.40 = f32[]{:T(128)} fusion(f32[128,8192]{1,0:T(8,128)} %get-tuple-element.10, f32[8192]{0:T(1024)S(1)} %broadcast_divide_fusion, f32[128]{0:T(128)S(1)} %copy-done.8), kind=kLoop, calls=%fused_computation.50 | loop fusion | flops 4194303 | bytes 4227588 | tf_op jit(solution)/shard_map/reduce_sum | solution.py:80
  309.3 5.4 %all-gather = f32[32768]{0:T(1024)S(1)} all-gather(f32[8192]{0:T(1024)S(1)} %broadcast_divide_fusion), channel_id=2, replica_groups=mesh['scen'=4,'var'=8] {'scen'}, dimensions={0}, use_global_device_ids=true | all-gather | bytes 163840 | tf_op jit(solution)/shard_map/all_gather | solution.py:82
  314.7 40.0 %all-reduce = (f32[]{:T(128)}, f32[]{:T(128)}) all-reduce(f32[]{:T(128)} %fusion.40, f32[]{:T(128)S(6)} %mul.145), channel_id=1, replica_groups=mesh['scen'=4,'var'=8] {'scen','var'}, use_global_device_ids=true, to_apply=%region_5.6 | all-reduce | flops 2 | bytes 16 | tf_op jit(solution)/shard_map/psum | solution.py:81
  356.3 6.1 %multiply_add_fusion = f32[128,8192]{1,0:T(8,128)} fusion(f32[128,8192]{1,0:T(8,128)} %param.10, f32[128,8192]{1,0:T(8,128)} %get-tuple-element.10, f32[]{:T(128)S(6)} %sqrt.11, f32[8192]{0:T(1024)S(1)} %broadcast_divide_fusion), kind=kLoop, calls=%fused_computation.51 | loop fusion | flops 3145728 | bytes 12615684 | tf_op jit(solution)/shard_map/add | solution.py:87
  (50 shorter events, 14.6 us)
Async XLA Ops:
  0.6 18.9 %copy-start.7 = (s32[128,64]{0,1:T(8,128)S(1)}, s32[128,64]{0,1:T(8,128)}, u32[]{:S(2)}) copy-start(s32[128,64]{0,1:T(8,128)} %param.17) | copy-start | bytes 98308
  0.6 27.2 %copy-start.6 = (f32[4,8192]{1,0:T(4,128)S(1)}, f32[4,8192]{1,0:T(4,128)}, u32[]{:S(2)}) copy-start(f32[4,8192]{1,0:T(4,128)} %param.16) | copy-start | bytes 393220
  8.3 9.4 %collective-permute-start = (f32[128,512]{1,0:T(8,128)S(1)}, f32[128,512]{1,0:T(8,128)S(1)}, u32[]{:S(2)}, u32[]{:S(2)}) collective-permute-start(f32[128,512]{1,0:T(8,128)S(1)} %fusion.55), channel_id=1, source_target_pairs={{0,1},{1,0},{2,3},{3,2},{4,5},{5,4},{6,7},{7,6},{8,9},{9,8},{10,11... | collective-permute-start | bytes 786440 | tf_op jit(solution)/shard_map/ppermute | solution.py:57
  17.7 7.5 %collective-permute-start.1 = (f32[128,512]{1,0:T(8,128)S(1)}, f32[128,512]{1,0:T(8,128)S(1)}, u32[]{:S(2)}, u32[]{:S(2)}) collective-permute-start(f32[128,512]{1,0:T(8,128)S(1)} %add.151), channel_id=1, source_target_pairs={{0,2},{1,3},{2,0},{3,1},{4,6},{5,7},{6,4},{7,5},{8,10},{9,11},{10,... | collective-permute-start | bytes 786440 | tf_op jit(solution)/shard_map/ppermute | solution.py:57
  25.2 16.0 %copy-start = (bf16[512,8192]{1,0:T(8,128)(2,1)S(1)}, bf16[512,8192]{1,0:T(8,128)(2,1)}, u32[]{:S(2)}) copy-start(bf16[512,8192]{1,0:T(8,128)(2,1)} %param.14) | copy-start | bytes 25165828
  25.2 16.0 %copy-start.2 = (bf16[128,8192]{1,0:T(8,128)(2,1)S(1)}, bf16[128,8192]{1,0:T(8,128)(2,1)}, u32[]{:S(2)}) copy-start(bf16[128,8192]{1,0:T(8,128)(2,1)} %param.12) | copy-start | bytes 6291460
  25.3 16.0 %copy-start.5 = (f32[128,512]{1,0:T(8,128)S(1)}, f32[128,512]{1,0:T(8,128)}, u32[]{:S(2)}) copy-start(f32[128,512]{1,0:T(8,128)} %param.13) | copy-start | bytes 786436
  25.3 13.2 %collective-permute-start.2 = (f32[128,512]{1,0:T(8,128)S(1)}, f32[128,512]{1,0:T(8,128)S(1)}, u32[]{:S(2)}, u32[]{:S(2)}) collective-permute-start(f32[128,512]{1,0:T(8,128)S(1)} %add.152), channel_id=1, source_target_pairs={{0,4},{1,5},{2,6},{3,7},{4,0},{5,1},{6,2},{7,3},{8,12},{9,13},{10,... | collective-permute-start | bytes 786440 | tf_op jit(solution)/shard_map/ppermute | solution.py:57
  33.1 220.7 %copy-start.1 = (f32[128,8192]{1,0:T(8,128)}, f32[128,8192]{1,0:T(8,128)S(1)}, u32[]{:S(2)}) copy-start(f32[128,8192]{1,0:T(8,128)S(1)} %convolution_subtract_fusion) | copy-start | bytes 12582916
  49.4 7.6 %collective-permute-start.3 = (f32[128,512]{1,0:T(8,128)S(1)}, f32[128,512]{1,0:T(8,128)S(1)}, u32[]{:S(2)}, u32[]{:S(2)}) collective-permute-start(f32[128,512]{1,0:T(8,128)S(1)} %fusion.53), channel_id=1, source_target_pairs={{0,1},{1,0},{2,3},{3,2},{4,5},{5,4},{6,7},{7,6},{8,9},{9,8},{10,11... | collective-permute-start | bytes 786440 | tf_op jit(solution)/shard_map/ppermute | solution.py:57
  57.0 6.8 %collective-permute-start.4 = (f32[128,512]{1,0:T(8,128)S(1)}, f32[128,512]{1,0:T(8,128)S(1)}, u32[]{:S(2)}, u32[]{:S(2)}) collective-permute-start(f32[128,512]{1,0:T(8,128)S(1)} %add.156), channel_id=1, source_target_pairs={{0,2},{1,3},{2,0},{3,1},{4,6},{5,7},{6,4},{7,5},{8,10},{9,11},{10,... | collective-permute-start | bytes 786440 | tf_op jit(solution)/shard_map/ppermute | solution.py:57
  63.8 14.1 %collective-permute-start.5 = (f32[128,512]{1,0:T(8,128)S(1)}, f32[128,512]{1,0:T(8,128)S(1)}, u32[]{:S(2)}, u32[]{:S(2)}) collective-permute-start(f32[128,512]{1,0:T(8,128)S(1)} %add.157), channel_id=1, source_target_pairs={{0,4},{1,5},{2,6},{3,7},{4,0},{5,1},{6,2},{7,3},{8,12},{9,13},{10,... | collective-permute-start | bytes 786440 | tf_op jit(solution)/shard_map/ppermute | solution.py:57
  84.2 7.4 %collective-permute-start.6 = (f32[128,512]{1,0:T(8,128)S(1)}, f32[128,512]{1,0:T(8,128)S(1)}, u32[]{:S(2)}, u32[]{:S(2)}) collective-permute-start(f32[128,512]{1,0:T(8,128)S(1)} %fusion.51), channel_id=1, source_target_pairs={{0,1},{1,0},{2,3},{3,2},{4,5},{5,4},{6,7},{7,6},{8,9},{9,8},{10,11... | collective-permute-start | bytes 786440 | tf_op jit(solution)/shard_map/ppermute | solution.py:57
  91.6 7.3 %collective-permute-start.7 = (f32[128,512]{1,0:T(8,128)S(1)}, f32[128,512]{1,0:T(8,128)S(1)}, u32[]{:S(2)}, u32[]{:S(2)}) collective-permute-start(f32[128,512]{1,0:T(8,128)S(1)} %add.161), channel_id=1, source_target_pairs={{0,2},{1,3},{2,0},{3,1},{4,6},{5,7},{6,4},{7,5},{8,10},{9,11},{10,... | collective-permute-start | bytes 786440 | tf_op jit(solution)/shard_map/ppermute | solution.py:57
  98.9 14.1 %collective-permute-start.8 = (f32[128,512]{1,0:T(8,128)S(1)}, f32[128,512]{1,0:T(8,128)S(1)}, u32[]{:S(2)}, u32[]{:S(2)}) collective-permute-start(f32[128,512]{1,0:T(8,128)S(1)} %add.162), channel_id=1, source_target_pairs={{0,4},{1,5},{2,6},{3,7},{4,0},{5,1},{6,2},{7,3},{8,12},{9,13},{10,... | collective-permute-start | bytes 786440 | tf_op jit(solution)/shard_map/ppermute | solution.py:57
  119.4 7.4 %collective-permute-start.9 = (f32[128,512]{1,0:T(8,128)S(1)}, f32[128,512]{1,0:T(8,128)S(1)}, u32[]{:S(2)}, u32[]{:S(2)}) collective-permute-start(f32[128,512]{1,0:T(8,128)S(1)} %fusion.49), channel_id=1, source_target_pairs={{0,1},{1,0},{2,3},{3,2},{4,5},{5,4},{6,7},{7,6},{8,9},{9,8},{10,11... | collective-permute-start | bytes 786440 | tf_op jit(solution)/shard_map/ppermute | solution.py:57
  126.9 7.3 %collective-permute-start.10 = (f32[128,512]{1,0:T(8,128)S(1)}, f32[128,512]{1,0:T(8,128)S(1)}, u32[]{:S(2)}, u32[]{:S(2)}) collective-permute-start(f32[128,512]{1,0:T(8,128)S(1)} %add.166), channel_id=1, source_target_pairs={{0,2},{1,3},{2,0},{3,1},{4,6},{5,7},{6,4},{7,5},{8,10},{9,11},{10,... | collective-permute-start | bytes 786440 | tf_op jit(solution)/shard_map/ppermute | solution.py:57
  134.2 14.1 %collective-permute-start.11 = (f32[128,512]{1,0:T(8,128)S(1)}, f32[128,512]{1,0:T(8,128)S(1)}, u32[]{:S(2)}, u32[]{:S(2)}) collective-permute-start(f32[128,512]{1,0:T(8,128)S(1)} %add.167), channel_id=1, source_target_pairs={{0,4},{1,5},{2,6},{3,7},{4,0},{5,1},{6,2},{7,3},{8,12},{9,13},{10,... | collective-permute-start | bytes 786440 | tf_op jit(solution)/shard_map/ppermute | solution.py:57
  154.5 7.4 %collective-permute-start.12 = (f32[128,512]{1,0:T(8,128)S(1)}, f32[128,512]{1,0:T(8,128)S(1)}, u32[]{:S(2)}, u32[]{:S(2)}) collective-permute-start(f32[128,512]{1,0:T(8,128)S(1)} %fusion.47), channel_id=1, source_target_pairs={{0,1},{1,0},{2,3},{3,2},{4,5},{5,4},{6,7},{7,6},{8,9},{9,8},{10,11... | collective-permute-start | bytes 786440 | tf_op jit(solution)/shard_map/ppermute | solution.py:57
  161.9 7.3 %collective-permute-start.13 = (f32[128,512]{1,0:T(8,128)S(1)}, f32[128,512]{1,0:T(8,128)S(1)}, u32[]{:S(2)}, u32[]{:S(2)}) collective-permute-start(f32[128,512]{1,0:T(8,128)S(1)} %add.171), channel_id=1, source_target_pairs={{0,2},{1,3},{2,0},{3,1},{4,6},{5,7},{6,4},{7,5},{8,10},{9,11},{10,... | collective-permute-start | bytes 786440 | tf_op jit(solution)/shard_map/ppermute | solution.py:57
  169.3 14.1 %collective-permute-start.14 = (f32[128,512]{1,0:T(8,128)S(1)}, f32[128,512]{1,0:T(8,128)S(1)}, u32[]{:S(2)}, u32[]{:S(2)}) collective-permute-start(f32[128,512]{1,0:T(8,128)S(1)} %add.172), channel_id=1, source_target_pairs={{0,4},{1,5},{2,6},{3,7},{4,0},{5,1},{6,2},{7,3},{8,12},{9,13},{10,... | collective-permute-start | bytes 786440 | tf_op jit(solution)/shard_map/ppermute | solution.py:57
  189.6 7.4 %collective-permute-start.15 = (f32[128,512]{1,0:T(8,128)S(1)}, f32[128,512]{1,0:T(8,128)S(1)}, u32[]{:S(2)}, u32[]{:S(2)}) collective-permute-start(f32[128,512]{1,0:T(8,128)S(1)} %fusion.45), channel_id=1, source_target_pairs={{0,1},{1,0},{2,3},{3,2},{4,5},{5,4},{6,7},{7,6},{8,9},{9,8},{10,11... | collective-permute-start | bytes 786440 | tf_op jit(solution)/shard_map/ppermute | solution.py:57
  197.0 7.3 %collective-permute-start.16 = (f32[128,512]{1,0:T(8,128)S(1)}, f32[128,512]{1,0:T(8,128)S(1)}, u32[]{:S(2)}, u32[]{:S(2)}) collective-permute-start(f32[128,512]{1,0:T(8,128)S(1)} %add.176), channel_id=1, source_target_pairs={{0,2},{1,3},{2,0},{3,1},{4,6},{5,7},{6,4},{7,5},{8,10},{9,11},{10,... | collective-permute-start | bytes 786440 | tf_op jit(solution)/shard_map/ppermute | solution.py:57
  204.4 14.1 %collective-permute-start.17 = (f32[128,512]{1,0:T(8,128)S(1)}, f32[128,512]{1,0:T(8,128)S(1)}, u32[]{:S(2)}, u32[]{:S(2)}) collective-permute-start(f32[128,512]{1,0:T(8,128)S(1)} %add.177), channel_id=1, source_target_pairs={{0,4},{1,5},{2,6},{3,7},{4,0},{5,1},{6,2},{7,3},{8,12},{9,13},{10,... | collective-permute-start | bytes 786440 | tf_op jit(solution)/shard_map/ppermute | solution.py:57
  222.0 21.2 %copy-start.4 = (f32[128,8192]{1,0:T(8,128)}, f32[128,8192]{1,0:T(8,128)S(1)}, u32[]{:S(2)}) copy-start(f32[128,8192]{1,0:T(8,128)S(1)} %fusion.29) | copy-start | bytes 12582916
  224.9 7.4 %collective-permute-start.18 = (f32[128,512]{1,0:T(8,128)S(1)}, f32[128,512]{1,0:T(8,128)S(1)}, u32[]{:S(2)}, u32[]{:S(2)}) collective-permute-start(f32[128,512]{1,0:T(8,128)S(1)} %fusion.43), channel_id=1, source_target_pairs={{0,1},{1,0},{2,3},{3,2},{4,5},{5,4},{6,7},{7,6},{8,9},{9,8},{10,11... | collective-permute-start | bytes 786440 | tf_op jit(solution)/shard_map/ppermute | solution.py:57
  232.4 7.3 %collective-permute-start.19 = (f32[128,512]{1,0:T(8,128)S(1)}, f32[128,512]{1,0:T(8,128)S(1)}, u32[]{:S(2)}, u32[]{:S(2)}) collective-permute-start(f32[128,512]{1,0:T(8,128)S(1)} %add.181), channel_id=1, source_target_pairs={{0,2},{1,3},{2,0},{3,1},{4,6},{5,7},{6,4},{7,5},{8,10},{9,11},{10,... | collective-permute-start | bytes 786440 | tf_op jit(solution)/shard_map/ppermute | solution.py:57
  239.7 14.1 %collective-permute-start.20 = (f32[128,512]{1,0:T(8,128)S(1)}, f32[128,512]{1,0:T(8,128)S(1)}, u32[]{:S(2)}, u32[]{:S(2)}) collective-permute-start(f32[128,512]{1,0:T(8,128)S(1)} %add.182), channel_id=1, source_target_pairs={{0,4},{1,5},{2,6},{3,7},{4,0},{5,1},{6,2},{7,3},{8,12},{9,13},{10,... | collective-permute-start | bytes 786440 | tf_op jit(solution)/shard_map/ppermute | solution.py:57
  258.6 3.0 copy-start.3
  258.6 21.8 %copy-start.8 = (f32[128]{0:T(128)S(1)}, f32[128]{0:T(128)}, u32[]{:S(2)}) copy-start(f32[128]{0:T(128)} %param.15) | copy-start | bytes 1540
  261.5 7.4 %collective-permute-start.21 = (f32[128,512]{1,0:T(8,128)S(1)}, f32[128,512]{1,0:T(8,128)S(1)}, u32[]{:S(2)}, u32[]{:S(2)}) collective-permute-start(f32[128,512]{1,0:T(8,128)S(1)} %fusion.41), channel_id=1, source_target_pairs={{0,1},{1,0},{2,3},{3,2},{4,5},{5,4},{6,7},{7,6},{8,9},{9,8},{10,11... | collective-permute-start | bytes 786440 | tf_op jit(solution)/shard_map/ppermute | solution.py:57
  269.0 7.3 %collective-permute-start.22 = (f32[128,512]{1,0:T(8,128)S(1)}, f32[128,512]{1,0:T(8,128)S(1)}, u32[]{:S(2)}, u32[]{:S(2)}) collective-permute-start(f32[128,512]{1,0:T(8,128)S(1)} %add.186), channel_id=1, source_target_pairs={{0,2},{1,3},{2,0},{3,1},{4,6},{5,7},{6,4},{7,5},{8,10},{9,11},{10,... | collective-permute-start | bytes 786440 | tf_op jit(solution)/shard_map/ppermute | solution.py:57
  277.0 14.4 %collective-permute-start.23 = (f32[128,512]{1,0:T(8,128)}, f32[128,512]{1,0:T(8,128)}, u32[]{:S(2)}, u32[]{:S(2)}) collective-permute-start(f32[128,512]{1,0:T(8,128)} %add.187), channel_id=1, source_target_pairs={{0,4},{1,5},{2,6},{3,7},{4,0},{5,1},{6,2},{7,3},{8,12},{9,13},{10,... | collective-permute-start | bytes 786440 | tf_op jit(solution)/shard_map/ppermute | solution.py:57
